TPU v7x, 32 devices: a whole 2x2x4 slice. The times are simulated.
32 devices in a mesh: sweep: 2 (over y), row: 4 (over z), col: 2 (over x), dp: 2 (over core).
Axes of the slice: x: 2, y: 2, z: 4, core: 2. Of those that a mesh axis runs over, the one named last changes fastest.
Arguments:
- token_ids: int32 [4096], P(('sweep', 'dp')), parts along dimension 0, may hold values from 0 to 15999
- sweep_index: int32 [4], P('sweep'), parts along dimension 0, may hold values from 0 to 7
- table: bfloat16 [16000, 4096], P('row', 'col'), may hold values from -6 to 6
- cotangent: bfloat16 [4096, 4096], P(('sweep', 'dp', 'row'), 'col'), parts along dimension 0, may hold values from -0.13183594 to 0.13183594
- gate_weight: bfloat16 [4096, 11008], P('col', 'row'), may hold values from -0.09375 to 0.09375
- up_weight: bfloat16 [4096, 11008], P('col', 'row'), may hold values from -0.09375 to 0.09375
- down_weight: bfloat16 [11008, 4096], P('row', 'col'), may hold values from -0.0546875 to 0.0546875
Outputs:
- grad_gate: float32 [8192, 11008], P(('sweep', 'col'), ('row', 'dp')), parts along dimension 0
- grad_up: float32 [8192, 11008], P(('sweep', 'col'), ('row', 'dp')), parts along dimension 0
- grad_down: float32 [22016, 4096], P(('sweep', 'row'), ('col', 'dp')), parts along dimension 0
There are 2 independent parts, one for each index of `sweep`. A program takes and returns all parts, laid end to end along the dimension named above; an argument that names none is the same for every part. Nothing has to cross between parts.
All inputs are finite; a program needn't handle non-finite values.
Results may differ from a plain program's by a relative error of at most 0.0062.
Values may be sent and summed in bfloat16 or wider, within the bound.
A program may use at most 256 MiB of HBM per device.

v0:
```python
import jax
import jax.numpy as jnp
from jax import lax
from jax.sharding import PartitionSpec as P


def contract_rows(left, right):
    return lax.dot_general(
        left, right, (((0,), (0,)), ((), ())), preferred_element_type=jnp.float32
    )


def contract_cols(left, right):
    return lax.dot_general(
        left, right, (((1,), (1,)), ((), ())), preferred_element_type=jnp.float32
    )


def local(token_ids, sweep_index, table, cotangent, gate_weight, up_weight, down_weight):
    k_input = sweep_index[0].astype(jnp.float32)
    k_output = sweep_index[1].astype(jnp.float32)
    in_mult = jnp.exp2(k_input / 2.0 - 1.5)
    out_mult = jnp.exp2(1.0 - k_output / 2.0)
    table_rows = table.shape[0]
    offset = token_ids - lax.axis_index("row") * table_rows
    inside = jnp.logical_and(offset >= 0, offset < table_rows)
    picked = jnp.take(table, jnp.clip(offset, 0, table_rows - 1), axis=0)
    looked = jnp.where(inside[:, None], picked, jnp.zeros((), jnp.bfloat16))
    embedded = lax.psum(looked, "row").astype(jnp.float32)
    scaled = (in_mult * embedded).astype(jnp.bfloat16)
    grads_rows = lax.all_gather(cotangent, "row", axis=0, tiled=True)
    width = gate_weight.shape[1]
    x_rows = scaled
    d_rows = grads_rows
    gate_part = jnp.dot(x_rows, gate_weight, preferred_element_type=jnp.float32)
    up_part = jnp.dot(x_rows, up_weight, preferred_element_type=jnp.float32)
    back_part = contract_cols(d_rows, down_weight)
    mixed = lax.psum_scatter(
        jnp.concatenate([gate_part, up_part, back_part], axis=1),
        "col",
        scatter_dimension=0,
        tiled=True,
    )
    gate = mixed[:, :width]
    up = mixed[:, width : 2 * width]
    back = mixed[:, 2 * width :]
    back = out_mult * back
    sig = jax.nn.sigmoid(gate)
    silu = gate * sig
    hidden = (silu * up).astype(jnp.bfloat16)
    d_gate = (back * up * sig * (1.0 + gate * (1.0 - sig))).astype(jnp.bfloat16)
    d_up = (back * silu).astype(jnp.bfloat16)
    x_rows = scaled
    d_rows = grads_rows
    acc_down = contract_rows(lax.all_gather(hidden, "col", axis=0, tiled=True), d_rows)
    acc_gate = contract_rows(x_rows, lax.all_gather(d_gate, "col", axis=0, tiled=True))
    acc_up = contract_rows(x_rows, lax.all_gather(d_up, "col", axis=0, tiled=True))
    acc_down, acc_gate, acc_up = (acc_down, acc_gate, acc_up)
    acc_down = out_mult * acc_down
    grad_gate, grad_up, grad_down = (
        lax.psum_scatter(acc_gate, "dp", scatter_dimension=1, tiled=True),
        lax.psum_scatter(acc_up, "dp", scatter_dimension=1, tiled=True),
        lax.psum_scatter(acc_down, "dp", scatter_dimension=1, tiled=True),
    )
    return (grad_gate, grad_up, grad_down)


def solution(mesh):
    return jax.shard_map(
        local,
        mesh=mesh,
        in_specs=(
            P(("sweep", "dp")),
            P("sweep"),
            P("row", "col"),
            P(("sweep", "dp", "row"), "col"),
            P("col", "row"),
            P("col", "row"),
            P("row", "col"),
        ),
        out_specs=(
            P(("sweep", "col"), ("row", "dp")),
            P(("sweep", "col"), ("row", "dp")),
            P(("sweep", "row"), ("col", "dp")),
        ),
        check_vma=False,
    )
```

profile of v0, /device:TPU:0, one launch (start us, length us, event | category | flops | bytes accessed | tf_op | source)
XLA Modules:
  0.0 1019.8 jit_solution(16046031713710483176)
XLA Ops:
  7.2 0.7 compare_and_fusion.1
  7.9 0.7 fusion.5
  8.6 16.6 %gather_fusion = bf16[1024,2048]{1,0:T(8,128)(2,1)} fusion(bf16[4000,2048]{1,0:T(8,128)(2,1)} %param.9, s32[1024]{0:T(1024)S(1)} %fusion.5), kind=kCustom, calls=%fused_computation | custom fusion | bytes 8392704 | tf_op jit(solution)/shard_map/jit(_take)/gather | solution.py:27
  25.2 4.1 select_select_fusion
  29.4 0.7 all-gather.5.cloned.1.call-update
  30.4 0.6 fusion.6
  31.8 155.4 %all-reduce.2.cloned.1.call-done = bf16[1024,2048]{1,0:T(8,128)(2,1)} async-done(((bf16[1024,2048]{1,0:T(8,128)(2,1)}), bf16[1024,2048]{1,0:T(8,128)(2,1)}) %all-reduce.2.cloned.1.call-update) | async-done | bytes 4194320 | tf_op jit(solution)/shard_map/psum | solution.py:29
  187.2 17.7 %fusion.3 = f32[1024,2752]{0,1:T(8,128)} fusion(bf16[2048,2752]{0,1:T(8,128)(2,1)} %param.12, bf16[1024,2048]{1,0:T(8,128)(2,1)} %all-reduce.2.cloned.1.call-done, f32[]{:T(128)} %bitcast), kind=kOutput, calls=%fused_computation.13 | convolution fusion | flops 11549016064 | bytes 26738692 | tf_op jit(solution)/shard_map/dot_general | solution.py:36
  204.9 14.8 %fusion.4 = f32[1024,2752]{0,1:T(8,128)} fusion(bf16[2048,2752]{0,1:T(8,128)(2,1)S(1)} %bitcast.11, bf16[1024,2048]{1,0:T(8,128)(2,1)S(1)} %copy-done.3, f32[]{:T(128)} %bitcast), kind=kOutput, calls=%fused_computation.14 | convolution fusion | flops 11549016064 | bytes 26738692 | tf_op jit(solution)/shard_map/dot_general | solution.py:35
  219.7 48.8 %all-gather.5.cloned.1.call-done = bf16[1024,2048]{1,0:T(8,128)(2,1)} async-done(((bf16[256,2048]{1,0:T(8,128)(2,1)}), bf16[1024,2048]{1,0:T(8,128)(2,1)}) %all-gather.5.cloned.1.call-update) | async-done | bytes 4194320 | tf_op jit(solution)/shard_map/all_gather | solution.py:31
  268.5 18.3 %fusion.7 = f32[1024,2752]{0,1:T(8,128)} fusion(bf16[1024,2048]{1,0:T(8,128)(2,1)} %all-gather.5.cloned.1.call-done, bf16[2752,2048]{1,0:T(8,128)(2,1)} %param.13), kind=kOutput, calls=%fused_computation.20 | convolution fusion | flops 11542724608 | bytes 26738688 | tf_op jit(solution)/shard_map/dot_general | solution.py:14
  286.8 24.1 %pad_maximum_fusion = f32[1024,8256]{0,1:T(8,128)} fusion(f32[1024,2752]{0,1:T(8,128)} %fusion.7, f32[1024,2752]{0,1:T(8,128)S(1)} %copy-done, f32[1024,2752]{0,1:T(8,128)S(1)} %copy-done.1), kind=kLoop, calls=%fused_computation.1 | loop fusion | flops 16908288 | bytes 67633152 | tf_op jit(solution)/shard_map/concatenate | solution.py:39
  311.6 369.6 %reduce-scatter.5.cloned.1.call-done = f32[512,8256]{0,1:T(8,128)} async-done(((f32[1024,8256]{0,1:T(8,128)}), f32[512,8256]{0,1:T(8,128)}) %reduce-scatter.5.cloned.1.call-update) | async-done | bytes 16908304 | tf_op jit(solution)/shard_map/reduce_scatter | solution.py:38
  681.3 10.8 %multiply_convert_fusion.1 = (bf16[512,2752]{0,1:T(8,128)(2,1)}, bf16[512,2752]{0,1:T(8,128)(2,1)}, bf16[512,2752]{0,1:T(8,128)(2,1)}) fusion(f32[512,8256]{0,1:T(8,128)} %reduce-scatter.5.cloned.1.call-done, f32[]{:T(128)} %bitcast.1), kind=kLoop, calls=%fused_computation.5 | loop fusion | flops 22544384 | bytes 25362436 | tf_op jit(solution)/shard_map/convert_element_type | solution.py:50
  692.2 0.5 all-gather.9.cloned.1.call-update
  693.4 71.9 %all-gather.11.cloned.1.call-done = bf16[1024,2752]{0,1:T(8,128)(2,1)} async-done(((bf16[512,2752]{0,1:T(8,128)(2,1)}), bf16[1024,2752]{0,1:T(8,128)(2,1)}) %all-gather.11.cloned.1.call-update) | async-done | bytes 5636112 | tf_op jit(solution)/shard_map/all_gather | solution.py:55
  765.3 19.4 %convolution_multiply_fusion = f32[2752,2048]{1,0:T(8,128)} fusion(bf16[1024,2752]{0,1:T(8,128)(2,1)} %all-gather.11.cloned.1.call-done, bf16[1024,2048]{1,0:T(8,128)(2,1)} %all-gather.5.cloned.1.call-done, f32[]{:T(128)} %bitcast.1), kind=kOutput, calls=%fused_computation.2 | convolution fusion | flops 11548360704 | bytes 32374788 | tf_op jit(solution)/shard_map/dot_general | solution.py:8
  784.7 55.5 %all-gather.9.cloned.1.call-done = bf16[1024,2752]{0,1:T(8,128)(2,1)} async-done(((bf16[512,2752]{0,1:T(8,128)(2,1)}), bf16[1024,2752]{0,1:T(8,128)(2,1)}) %all-gather.9.cloned.1.call-update) | async-done | bytes 5636112 | tf_op jit(solution)/shard_map/all_gather | solution.py:57
  840.3 19.3 %fusion.2 = f32[2048,2752]{0,1:T(8,128)} fusion(bf16[1024,2752]{0,1:T(8,128)(2,1)} %all-gather.9.cloned.1.call-done, bf16[1024,2048]{1,0:T(8,128)(2,1)} %all-reduce.2.cloned.1.call-done, f32[]{:T(128)} %bitcast), kind=kOutput, calls=%fused_computation.12 | convolution fusion | flops 11549016064 | bytes 32374788 | tf_op jit(solution)/shard_map/dot_general | solution.py:8
  859.6 55.6 %all-gather.7.cloned.1.call-done = bf16[1024,2752]{0,1:T(8,128)(2,1)} async-done(((bf16[512,2752]{0,1:T(8,128)(2,1)}), bf16[1024,2752]{0,1:T(8,128)(2,1)}) %all-gather.7.cloned.1.call-update) | async-done | bytes 5636112 | tf_op jit(solution)/shard_map/all_gather | solution.py:56
  915.2 23.9 %fusion.1 = f32[2048,2752]{0,1:T(8,128)} fusion(bf16[1024,2752]{0,1:T(8,128)(2,1)} %all-gather.7.cloned.1.call-done, bf16[1024,2048]{1,0:T(8,128)(2,1)} %all-reduce.2.cloned.1.call-done, f32[]{:T(128)} %bitcast), kind=kOutput, calls=%fused_computation.11 | convolution fusion | flops 11549016064 | bytes 32374788 | tf_op jit(solution)/shard_map/dot_general | solution.py:8
  939.2 7.7 reduce-scatter.11.cloned.1.call-done
  946.8 33.1 %reduce-scatter.9.cloned.1.call-done = f32[2048,1376]{0,1:T(8,128)} async-done(((f32[2048,2752]{0,1:T(8,128)}), f32[2048,1376]{0,1:T(8,128)}) %reduce-scatter.9.cloned.1.call-update) | async-done | bytes 11272208 | tf_op jit(solution)/shard_map/reduce_scatter | solution.py:62
  980.0 33.1 %reduce-scatter.7.cloned.1.call-done = f32[2048,1376]{0,1:T(8,128)} async-done(((f32[2048,2752]{0,1:T(8,128)}), f32[2048,1376]{0,1:T(8,128)}) %reduce-scatter.7.cloned.1.call-update) | async-done | bytes 11272208 | tf_op jit(solution)/shard_map/reduce_scatter | solution.py:61
  (31 shorter events, 1.3 us)
Async XLA Ops:
  7.2 180.0 %all-reduce.2.cloned.1.call-start = ((), (), s32[]{:S(2)}) async-start(), calls=%async_computation.4 | async-start | bytes 8388608 | tf_op jit(solution)/shard_map/psum | solution.py:29
  25.2 5.2 copy-start.2
  29.3 175.6 %slice-start = ((s8[11272192]{0:T(1024)(128)(4,1)}), s8[2883584]{0:T(1024)(128)(4,1)S(1)}, s32[]{:S(2)}) async-start(s8[11272192]{0:T(1024)(128)(4,1)} %bitcast.10), calls=%async_computation.13 | async-start | bytes 5767168
  29.3 239.2 %all-gather.5.cloned.1.call-start = ((), (), s32[]{:S(2)}) async-start(), calls=%async_computation.5 | async-start | bytes 5242880 | tf_op jit(solution)/shard_map/all_gather | solution.py:31
  30.1 651.2 %reduce-scatter.5.cloned.1.call-start = ((), (), s32[]{:S(2)}) async-start(), calls=%async_computation.6 | async-start | bytes 50724864 | tf_op jit(solution)/shard_map/reduce_scatter | solution.py:38
  187.2 17.7 %slice-start.1 = ((s8[11272192]{0:T(1024)(128)(4,1)}), s8[4194304]{0:T(1024)(128)(4,1)S(1)}, s32[]{:S(2)}) async-start(s8[11272192]{0:T(1024)(128)(4,1)} %bitcast.10), calls=%async_computation.14 | async-start | bytes 8388608
  187.2 17.7 %slice-start.2 = ((s8[11272192]{0:T(1024)(128)(4,1)}), s8[4194304]{0:T(1024)(128)(4,1)S(1)}, s32[]{:S(2)}) async-start(s8[11272192]{0:T(1024)(128)(4,1)} %bitcast.10), calls=%async_computation.15 | async-start | bytes 8388608
  187.2 17.7 %copy-start.3 = (bf16[1024,2048]{1,0:T(8,128)(2,1)S(1)}, bf16[1024,2048]{1,0:T(8,128)(2,1)}, u32[]{:S(2)}) copy-start(bf16[1024,2048]{1,0:T(8,128)(2,1)} %all-reduce.2.cloned.1.call-done) | copy-start | bytes 12582916
  268.5 18.3 %copy-start = (f32[1024,2752]{0,1:T(8,128)S(1)}, f32[1024,2752]{0,1:T(8,128)}, u32[]{:S(2)}) copy-start(f32[1024,2752]{0,1:T(8,128)} %fusion.3) | copy-start | bytes 33816580
  268.5 18.3 %copy-start.1 = (f32[1024,2752]{0,1:T(8,128)S(1)}, f32[1024,2752]{0,1:T(8,128)}, u32[]{:S(2)}) copy-start(f32[1024,2752]{0,1:T(8,128)} %fusion.4) | copy-start | bytes 33816580
  310.9 454.4 %all-gather.11.cloned.1.call-start = ((), (), s32[]{:S(2)}) async-start(), calls=%async_computation.11 | async-start | bytes 8454144 | tf_op jit(solution)/shard_map/all_gather | solution.py:55
  692.1 148.1 %all-gather.9.cloned.1.call-start = ((), (), s32[]{:S(2)}) async-start(), calls=%async_computation.9 | async-start | bytes 8454144 | tf_op jit(solution)/shard_map/all_gather | solution.py:57
  692.7 222.5 %all-gather.7.cloned.1.call-start = ((), (), s32[]{:S(2)}) async-start(), calls=%async_computation.7 | async-start | bytes 8454144 | tf_op jit(solution)/shard_map/all_gather | solution.py:56
  693.3 253.5 %reduce-scatter.11.cloned.1.call-start = ((), (), s32[]{:S(2)}) async-start(), calls=%async_computation.12 | async-start | bytes 33816576 | tf_op jit(solution)/shard_map/reduce_scatter | solution.py:63
  784.7 195.3 %reduce-scatter.9.cloned.1.call-start = ((), (), s32[]{:S(2)}) async-start(), calls=%async_computation.10 | async-start | bytes 33816576 | tf_op jit(solution)/shard_map/reduce_scatter | solution.py:62
  859.5 153.5 %reduce-scatter.7.cloned.1.call-start = ((), (), s32[]{:S(2)}) async-start(), calls=%async_computation.8 | async-start | bytes 33816576 | tf_op jit(solution)/shard_map/reduce_scatter | solution.py:61
Sparse Core Ops, SparseCore 0:
  29.4 157.6 all-reduce.1
  188.8 79.6 all-gather.4
  311.0 370.2 reduce-scatter.4
  692.3 72.9 all-gather.10
  767.3 72.9 all-gather.8
  842.2 72.9 all-gather.6
  918.1 28.6 reduce-scatter.10
  949.7 30.1 reduce-scatter.8
  982.9 30.1 reduce-scatter.6
where the time goes:
time: 1020 us
  waiting for transfers between devices  833 us (82%)
  matrix products  113 us (11%)
  other arithmetic  40.4 us (4%)
  local copies, waits for them, and re-layouts  17.2 us (2%)
  between operations  15.5 us (2%)
    reduce_scatter x1, waiting for transfers between devices, local(): lax.psum_scatter(jnp.concatenate([gate_part, up_part, back_part], axis=1)...  370 us
    psum x1, waiting for transfers between devices, local(): embedded = lax.psum(looked, 'row').astype(jnp.float32)  155 us
    all_gather x1, waiting for transfers between devices, local(): lax.all_gather(hidden, 'col', axis=0, tiled=True)  71.9 us
    dot_general x3, matrix products, contract_rows(): lax.dot_general(left, right, (((0,), (0,)), ((), ())), preferred_element_...  62.5 us
    all_gather x1, waiting for transfers between devices, local(): lax.all_gather(d_gate, 'col', axis=0, tiled=True)  55.6 us
    all_gather x1, waiting for transfers between devices, local(): lax.all_gather(d_up, 'col', axis=0, tiled=True)  55.5 us
    all_gather x1, waiting for transfers between devices, local(): grads_rows = lax.all_gather(cotangent, 'row', axis=0, tiled=True)  48.8 us
    reduce_scatter x1, waiting for transfers between devices, local(): lax.psum_scatter(acc_gate, 'dp', scatter_dimension=1, tiled=True)  33.1 us
  transfers between devices with their start and end apart: 9, of which 9 were waited for; matrix products, arithmetic and copies ran while one was open for 9% of the time, Pallas kernels for 0%

commit v1 on v0

--- a/solution.py
+++ b/solution.py
@@ -26,7 +26,7 @@
     inside = jnp.logical_and(offset >= 0, offset < table_rows)
     picked = jnp.take(table, jnp.clip(offset, 0, table_rows - 1), axis=0)
     looked = jnp.where(inside[:, None], picked, jnp.zeros((), jnp.bfloat16))
-    embedded = lax.psum(looked, "row").astype(jnp.float32)
+    embedded = jnp.sum(lax.all_gather(looked, "row"), axis=0).astype(jnp.float32)
     scaled = (in_mult * embedded).astype(jnp.bfloat16)
     grads_rows = lax.all_gather(cotangent, "row", axis=0, tiled=True)
     width = gate_weight.shape[1]

time: 1020 us -> 1160 us (1.14)
  waiting for transfers between devices: 833 us -> 959 us
  other arithmetic: 40.4 us -> 53.6 us
    all_gather x0 -> x1, waiting for transfers between devices: none -> 270 us  [local(): lax.all_gather(looked, 'row')]
    psum x1 -> x0, waiting for transfers between devices: 155 us -> none  [local(): embedded = lax.psum(looked, 'row').astype(jnp.float32)]
    all_gather x1, waiting for transfers between devices: 48.8 us -> 61.9 us  [local(): grads_rows = lax.all_gather(cotangent, 'row', axis=0, tiled=True)]
    reduce_sum x0 -> x1, other arithmetic: none -> 12.1 us  [local(): jnp.sum(lax.all_gather(looked, 'row'), axis=0).astype(jnp.float32)]
where the time goes in v1:
time: 1160 us
  waiting for transfers between devices  959 us (83%)
  matrix products  113 us (10%)
  other arithmetic  53.6 us (5%)
  local copies, waits for them, and re-layouts  17.3 us (1%)
  between operations  15.6 us (1%)
    reduce_scatter x1, waiting for transfers between devices, local(): lax.psum_scatter(jnp.concatenate([gate_part, up_part, back_part], axis=1)...  369 us
    all_gather x1, waiting for transfers between devices, local(): lax.all_gather(looked, 'row')  270 us
    all_gather x1, waiting for transfers between devices, local(): lax.all_gather(hidden, 'col', axis=0, tiled=True)  71.9 us
    dot_general x3, matrix products, contract_rows(): lax.dot_general(left, right, (((0,), (0,)), ((), ())), preferred_element_...  62.5 us
    all_gather x1, waiting for transfers between devices, local(): grads_rows = lax.all_gather(cotangent, 'row', axis=0, tiled=True)  61.9 us
    all_gather x1, waiting for transfers between devices, local(): lax.all_gather(d_up, 'col', axis=0, tiled=True)  55.5 us
    all_gather x1, waiting for transfers between devices, local(): lax.all_gather(d_gate, 'col', axis=0, tiled=True)  55.1 us
    reduce_scatter x1, waiting for transfers between devices, local(): lax.psum_scatter(acc_gate, 'dp', scatter_dimension=1, tiled=True)  33.1 us
  transfers between devices with their start and end apart: 9, of which 9 were waited for; matrix products, arithmetic and copies ran while one was open for 9% of the time, Pallas kernels for 0%

profile of v1, /device:TPU:0, one launch (start us, length us, event | category | flops | bytes accessed | tf_op | source)
XLA Modules:
  0.0 1159.8 jit_solution(1971199205998837749)
XLA Ops:
  7.2 0.7 all-gather.8.cloned.1.call-update
  8.0 0.7 fusion.6
  8.7 16.6 %gather_fusion = bf16[1024,2048]{1,0:T(8,128)(2,1)} fusion(bf16[4000,2048]{1,0:T(8,128)(2,1)} %param.9, s32[1024]{0:T(1024)S(1)} %fusion.6), kind=kCustom, calls=%fused_computation | custom fusion | bytes 8392704 | tf_op jit(solution)/shard_map/jit(_take)/gather | solution.py:27
  25.3 4.1 fusion.1
  29.8 0.6 fusion.7
  31.1 61.9 %all-gather.8.cloned.1.call-done = bf16[1024,2048]{1,0:T(8,128)(2,1)} async-done(((bf16[256,2048]{1,0:T(8,128)(2,1)}), bf16[1024,2048]{1,0:T(8,128)(2,1)}) %all-gather.8.cloned.1.call-update) | async-done | bytes 4194320 | tf_op jit(solution)/shard_map/all_gather | solution.py:31
  93.0 17.5 %fusion.8 = f32[1024,2752]{0,1:T(8,128)} fusion(bf16[1024,2048]{1,0:T(8,128)(2,1)} %all-gather.8.cloned.1.call-done, bf16[2752,2048]{1,0:T(8,128)(2,1)} %param.13), kind=kOutput, calls=%fused_computation.21 | convolution fusion | flops 11542724608 | bytes 26738688 | tf_op jit(solution)/shard_map/dot_general | solution.py:14
  110.5 269.9 %all-gather.6.cloned.1.call-done = bf16[4,1024,2048]{2,1,0:T(8,128)(2,1)} async-done(((bf16[1,1024,2048]{2,1,0:T(8,128)(2,1)}), bf16[4,1024,2048]{2,1,0:T(8,128)(2,1)}) %all-gather.6.cloned.1.call-update) | async-done | bytes 16777232 | tf_op jit(solution)/shard_map/all_gather | solution.py:29
  380.5 12.1 %reduce_sum.12 = bf16[1024,2048]{1,0:T(8,128)(2,1)} reduce(bf16[4,1024,2048]{2,1,0:T(8,128)(2,1)} %all-gather.6.cloned.1.call-done, bf16[]{:T(256)} %constant.46.clone.1), dimensions={0}, to_apply=%region_0.1 | reduce | flops 6291456 | bytes 20971522 | tf_op jit(solution)/shard_map/reduce_sum | solution.py:29
  392.6 16.1 %fusion.4 = f32[1024,2752]{0,1:T(8,128)S(1)} fusion(bf16[2048,2752]{0,1:T(8,128)(2,1)} %param.12, bf16[1024,2048]{1,0:T(8,128)(2,1)} %reduce_sum.12, f32[]{:T(128)} %bitcast), kind=kOutput, calls=%fused_computation.14 | convolution fusion | flops 11549016064 | bytes 26738692 | tf_op jit(solution)/shard_map/dot_general | solution.py:36
  408.7 17.1 %fusion.5 = f32[1024,2752]{0,1:T(8,128)} fusion(bf16[2048,2752]{0,1:T(8,128)(2,1)} %param.11, bf16[1024,2048]{1,0:T(8,128)(2,1)S(1)} %copy-done, f32[]{:T(128)} %bitcast), kind=kOutput, calls=%fused_computation.15 | convolution fusion | flops 11549016064 | bytes 26738692 | tf_op jit(solution)/shard_map/dot_general | solution.py:35
  425.8 25.9 %pad_maximum_fusion = f32[1024,8256]{0,1:T(8,128)} fusion(f32[1024,2752]{0,1:T(8,128)S(1)} %bitcast.15, f32[1024,2752]{0,1:T(8,128)S(1)} %fusion.4, f32[1024,2752]{0,1:T(8,128)} %fusion.5), kind=kLoop, calls=%fused_computation.1 | loop fusion | flops 16908288 | bytes 67633152 | tf_op jit(solution)/shard_map/concatenate | solution.py:39
  452.5 369.4 %reduce-scatter.5.cloned.1.call-done = f32[512,8256]{0,1:T(8,128)} async-done(((f32[1024,8256]{0,1:T(8,128)}), f32[512,8256]{0,1:T(8,128)}) %reduce-scatter.5.cloned.1.call-update) | async-done | bytes 16908304 | tf_op jit(solution)/shard_map/reduce_scatter | solution.py:38
  821.8 10.8 multiply_convert_fusion.1
  832.7 0.5 all-gather.12.cloned.1.call-update
  833.9 71.9 %all-gather.14.cloned.1.call-done = bf16[1024,2752]{0,1:T(8,128)(2,1)} async-done(((bf16[512,2752]{0,1:T(8,128)(2,1)}), bf16[1024,2752]{0,1:T(8,128)(2,1)}) %all-gather.14.cloned.1.call-update) | async-done | bytes 5636112 | tf_op jit(solution)/shard_map/all_gather | solution.py:55
  905.8 19.4 %convolution_multiply_fusion = f32[2752,2048]{1,0:T(8,128)} fusion(bf16[1024,2752]{0,1:T(8,128)(2,1)} %all-gather.14.cloned.1.call-done, bf16[1024,2048]{1,0:T(8,128)(2,1)} %all-gather.8.cloned.1.call-done, f32[]{:T(128)} %bitcast.2), kind=kOutput, calls=%fused_computation.2 | convolution fusion | flops 11548360704 | bytes 32374788 | tf_op jit(solution)/shard_map/dot_general | solution.py:8
  925.2 55.5 %all-gather.12.cloned.1.call-done = bf16[1024,2752]{0,1:T(8,128)(2,1)} async-done(((bf16[512,2752]{0,1:T(8,128)(2,1)}), bf16[1024,2752]{0,1:T(8,128)(2,1)}) %all-gather.12.cloned.1.call-update) | async-done | bytes 5636112 | tf_op jit(solution)/shard_map/all_gather | solution.py:57
  980.8 19.2 %fusion.3 = f32[2048,2752]{0,1:T(8,128)} fusion(bf16[1024,2752]{0,1:T(8,128)(2,1)} %all-gather.12.cloned.1.call-done, bf16[1024,2048]{1,0:T(8,128)(2,1)} %reduce_sum.12, f32[]{:T(128)} %bitcast), kind=kOutput, calls=%fused_computation.13 | convolution fusion | flops 11549016064 | bytes 32374788 | tf_op jit(solution)/shard_map/dot_general | solution.py:8
  1000.1 55.1 %all-gather.10.cloned.1.call-done = bf16[1024,2752]{0,1:T(8,128)(2,1)} async-done(((bf16[512,2752]{0,1:T(8,128)(2,1)}), bf16[1024,2752]{0,1:T(8,128)(2,1)}) %all-gather.10.cloned.1.call-update) | async-done | bytes 5636112 | tf_op jit(solution)/shard_map/all_gather | solution.py:56
  1055.2 23.9 %fusion.2 = f32[2048,2752]{0,1:T(8,128)} fusion(bf16[1024,2752]{0,1:T(8,128)(2,1)} %all-gather.10.cloned.1.call-done, bf16[1024,2048]{1,0:T(8,128)(2,1)} %reduce_sum.12, f32[]{:T(128)} %bitcast), kind=kOutput, calls=%fused_computation.12 | convolution fusion | flops 11549016064 | bytes 32374788 | tf_op jit(solution)/shard_map/dot_general | solution.py:8
  1079.1 7.7 reduce-scatter.11.cloned.1.call-done
  1086.8 33.1 %reduce-scatter.9.cloned.1.call-done = f32[2048,1376]{0,1:T(8,128)} async-done(((f32[2048,2752]{0,1:T(8,128)}), f32[2048,1376]{0,1:T(8,128)}) %reduce-scatter.9.cloned.1.call-update) | async-done | bytes 11272208 | tf_op jit(solution)/shard_map/reduce_scatter | solution.py:62
  1119.9 33.1 %reduce-scatter.7.cloned.1.call-done = f32[2048,1376]{0,1:T(8,128)} async-done(((f32[2048,2752]{0,1:T(8,128)}), f32[2048,1376]{0,1:T(8,128)}) %reduce-scatter.7.cloned.1.call-update) | async-done | bytes 11272208 | tf_op jit(solution)/shard_map/reduce_scatter | solution.py:61
  (30 shorter events, 1.3 us)
Async XLA Ops:
  7.2 85.9 %all-gather.8.cloned.1.call-start = ((), (), s32[]{:S(2)}) async-start(), calls=%async_computation.5 | async-start | bytes 5242880 | tf_op jit(solution)/shard_map/all_gather | solution.py:31
  7.9 372.6 %all-gather.6.cloned.1.call-start = ((), (), s32[]{:S(2)}) async-start(), calls=%async_computation.4 | async-start | bytes 20971520 | tf_op jit(solution)/shard_map/all_gather | solution.py:29
  8.6 16.6 %copy-start.1 = (s32[1024]{0:T(1024)S(1)}, s32[1024]{0:T(1024)}, u32[]{:S(2)}) copy-start(s32[1024]{0:T(1024)} %param.7) | copy-start | bytes 12292
  25.3 4.5 copy-start.2
  29.4 792.4 %reduce-scatter.5.cloned.1.call-start = ((), (), s32[]{:S(2)}) async-start(), calls=%async_computation.6 | async-start | bytes 50724864 | tf_op jit(solution)/shard_map/reduce_scatter | solution.py:38
  392.6 16.1 %copy-start = (bf16[1024,2048]{1,0:T(8,128)(2,1)S(1)}, bf16[1024,2048]{1,0:T(8,128)(2,1)}, u32[]{:S(2)}) copy-start(bf16[1024,2048]{1,0:T(8,128)(2,1)} %reduce_sum.12) | copy-start | bytes 12582916
  392.6 33.2 %slice-start = ((s8[11272192]{0:T(1024)(128)(4,1)}), s8[4194304]{0:T(1024)(128)(4,1)S(1)}, s32[]{:S(2)}) async-start(s8[11272192]{0:T(1024)(128)(4,1)} %bitcast.14), calls=%async_computation.13 | async-start | bytes 8388608
  392.6 33.2 %slice-start.1 = ((s8[11272192]{0:T(1024)(128)(4,1)}), s8[4194304]{0:T(1024)(128)(4,1)S(1)}, s32[]{:S(2)}) async-start(s8[11272192]{0:T(1024)(128)(4,1)} %bitcast.14), calls=%async_computation.14 | async-start | bytes 8388608
  408.7 17.1 %slice-start.2 = ((s8[11272192]{0:T(1024)(128)(4,1)}), s8[2883584]{0:T(1024)(128)(4,1)S(1)}, s32[]{:S(2)}) async-start(s8[11272192]{0:T(1024)(128)(4,1)} %bitcast.14), calls=%async_computation.15 | async-start | bytes 5767168
  451.7 454.1 %all-gather.14.cloned.1.call-start = ((), (), s32[]{:S(2)}) async-start(), calls=%async_computation.11 | async-start | bytes 8454144 | tf_op jit(solution)/shard_map/all_gather | solution.py:55
  832.7 148.1 %all-gather.12.cloned.1.call-start = ((), (), s32[]{:S(2)}) async-start(), calls=%async_computation.9 | async-start | bytes 8454144 | tf_op jit(solution)/shard_map/all_gather | solution.py:57
  833.3 221.9 %all-gather.10.cloned.1.call-start = ((), (), s32[]{:S(2)}) async-start(), calls=%async_computation.7 | async-start | bytes 8454144 | tf_op jit(solution)/shard_map/all_gather | solution.py:56
  833.8 252.9 %reduce-scatter.11.cloned.1.call-start = ((), (), s32[]{:S(2)}) async-start(), calls=%async_computation.12 | async-start | bytes 33816576 | tf_op jit(solution)/shard_map/reduce_scatter | solution.py:63
  925.2 194.7 %reduce-scatter.9.cloned.1.call-start = ((), (), s32[]{:S(2)}) async-start(), calls=%async_computation.10 | async-start | bytes 33816576 | tf_op jit(solution)/shard_map/reduce_scatter | solution.py:62
  1000.0 153.0 %reduce-scatter.7.cloned.1.call-start = ((), (), s32[]{:S(2)}) async-start(), calls=%async_computation.8 | async-start | bytes 33816576 | tf_op jit(solution)/shard_map/reduce_scatter | solution.py:61
Sparse Core Ops, SparseCore 0:
  9.5 83.4 all-gather.7
  95.2 285.2 all-gather.5
  451.8 369.9 reduce-scatter.4
  832.8 72.9 all-gather.13
  907.8 72.9 all-gather.11
  982.2 72.9 all-gather.9
  1058.1 28.6 reduce-scatter.10
  1089.7 30.1 reduce-scatter.8
  1122.8 30.1 reduce-scatter.6
